TPU v7x, 32 devices: a whole 2x2x4 slice. The times are simulated.
32 devices in a mesh: ma: 16 (over z, x, core), ba: 2 (over y).
Axes of the slice: x: 2, y: 2, z: 4, core: 2. Of those that a mesh axis runs over, the one named last changes fastest.
Arguments:
- fields: bfloat16 [4, 256, 256, 192], P('ba', 'ma'), may hold values from -6 to 6
- weight_real: bfloat16 [112, 64, 192, 192], P('ba', 'ma'), may hold values from -0.4375 to 0.4375
- weight_imag: bfloat16 [112, 64, 192, 192], P('ba', 'ma'), may hold values from -0.4375 to 0.4375
- skip_weight: bfloat16 [192, 192], replicated, may hold values from -0.4375 to 0.4375
- out_bias: float32 [192], replicated, may hold values from -3 to 3
Outputs:
- layer_out: bfloat16 [4, 256, 256, 192], P('ba', 'ma')
All inputs are finite; a program needn't handle non-finite values.
Results may differ from a plain program's by a relative error of at most 0.0095.
Values may be sent and summed in bfloat16 or wider, within the bound.
A program may use at most 128 MiB of HBM per device.

v0:
```python
import functools
import math

import jax
import jax.numpy as jnp
import numpy as np
from jax import lax
from jax.experimental import pallas as pl
from jax.experimental.pallas import tpu as pltpu
from jax.sharding import PartitionSpec as P

MESH = pl.DeviceIdType.MESH
BF = jnp.bfloat16
F32 = jnp.float32
LANES = 128
VMEM_LIMIT = 67043328


def angles(left, right, extent):
    turn = 2.0 * np.pi / extent * ((left[:, None] * right[None, :]) % extent)
    return np.cos(turn), np.sin(turn)


def packed_tables(H, W, KX, KY, n, nb):
    rows, cols, modes = H // n, KY // n, KX // nb
    s = 1.0 / math.sqrt(H * W)
    ky = np.arange(KY)
    cos_w, sin_w = angles(ky, np.arange(W), W)
    first = np.stack([cos_w * s, -sin_w * s], 1)
    first = first.reshape(n, cols, 2, W).transpose(1, 0, 2, 3).reshape(2 * KY, W)
    g = np.where(ky == 0, 1.0, 2.0)[:, None] * s
    last = np.stack([cos_w * g, -sin_w * g], 1)
    last = last.reshape(n, cols, 2, W).transpose(1, 0, 2, 3).reshape(2 * KY, W).T
    i = np.arange(KX)
    kx = np.where(i < KX // 2, i, i + H - KX)
    cos_h, sin_h = angles(kx, np.arange(H), H)
    down = np.stack([np.stack([cos_h, sin_h], 1), np.stack([-sin_h, cos_h], 1)], 0)
    down = down.reshape(2, nb, modes, 2, n, rows).transpose(1, 0, 2, 4, 3, 5)
    down = down.reshape(2 * KX, 2 * H)
    up = np.stack([np.stack([cos_h, -sin_h], 0), np.stack([sin_h, cos_h], 0)], 0)
    up = up.reshape(2, 2, nb, modes, n, rows).transpose(4, 0, 5, 2, 1, 3).reshape(2 * H, 2 * KX)
    return [jnp.asarray(a.astype(np.float32)).astype(BF) for a in (first, down, up, last)]


def dot(a, b):
    return jnp.dot(a, b, preferred_element_type=F32)


def spectral_kernel(
    n, nb, x_ref, wr_ref, wi_ref, first_ref, down_ref, up_ref, out_ref,
    colf, csend, crecv, ysend, yrecv, m1, m2, mo, zsend, zrecv, rsend, wbuf,
    csem_s, csem_r, ysem_s, ysem_r, zsem_s, zsem_r, rsem_s, rsem_r, wsem,
):
    bl, rows, W, C = x_ref.shape
    cols, _, rows2, L = csend.shape
    modes = wbuf.shape[2]
    K2 = first_ref.shape[0]
    tiles = L // LANES
    slots = wbuf.shape[0]
    group = 2 * nb * bl
    tail = C - LANES
    me = lax.axis_index("ma")
    mine = lax.axis_index("ba")

    def weights(q):
        s = q % slots
        return [
            pltpu.make_async_copy(ref.at[:, q], wbuf.at[s, p], wsem.at[s, p])
            for p, ref in enumerate((wr_ref, wi_ref))
        ]

    for q in range(min(slots, cols)):
        for copy in weights(q):
            copy.start()

    barrier = pltpu.get_barrier_semaphore()
    for j in range(1, n):
        pl.semaphore_signal(
            barrier, inc=1, device_id={"ma": lax.rem(me + j, n)}, device_id_type=MESH
        )
    for j in range(1, nb):
        pl.semaphore_signal(
            barrier, inc=1, device_id={"ba": lax.rem(mine + j, nb)}, device_id_type=MESH
        )

    def over_ma(src, dst, s, r, q, j):
        to = lax.rem(me + j, n)
        return pltpu.make_async_remote_copy(
            src_ref=src.at[q, to], dst_ref=dst.at[q, me], send_sem=s.at[q, j],
            recv_sem=r.at[q, j], device_id={"ma": to}, device_id_type=MESH,
        )

    def over_ba(src, dst, s, r, q, j):
        to = lax.rem(mine + j, nb)
        return pltpu.make_async_remote_copy(
            src_ref=src.at[q, to], dst_ref=dst.at[q, mine], send_sem=s.at[q, j],
            recv_sem=r.at[q, j], device_id={"ba": to}, device_id_type=MESH,
        )

    order = sorted(range(1, n), key=lambda j: -min(j, n - j))

    @pl.loop(0, rows)
    def _(h):
        parts = [dot(first_ref[...], x_ref[b, h]) for b in range(bl)]
        both = jnp.concatenate(parts, axis=1)
        for l in range(tiles):
            colf[l, pl.ds(pl.multiple_of(h * K2, K2), K2), :] = both[:, l * LANES:(l + 1) * LANES]

    sent = []
    for q in range(cols):
        @pl.loop(0, n)
        def _(d, q=q):
            for part in range(2):
                for l in range(tiles):
                    k = q * 2 * n + 2 * d + part
                    v = colf[l, pl.ds(k, rows, stride=K2), :]
                    csend[q, d, part * rows:(part + 1) * rows, l * LANES:(l + 1) * LANES] = v.astype(BF)

        crecv[q, me] = csend[q, me]
        if q == 0:
            pl.semaphore_wait(barrier, n - 1 + nb - 1)
        for j in order:
            c = over_ma(csend, crecv, csem_s, csem_r, q, j)
            c.start()
            sent.append(c)

    ysent, zsent = {}, {}

    def rows_down(q):
        for j in order:
            over_ma(csend, crecv, csem_s, csem_r, q, j).wait_recv()
        col = crecv[q].reshape(n * rows2, L)
        spec = dot(down_ref[...], col).astype(BF)
        for y in range(nb):
            ysend[q, y] = spec[y * 2 * modes:(y + 1) * 2 * modes]
        for j in range(1, nb):
            c = over_ba(ysend, yrecv, ysem_s, ysem_r, q, j)
            c.start()
            sent.append(c)
        yrecv[q, mine] = ysend[q, mine]

    def mix(q):
        for j in range(1, nb):
            over_ba(ysend, yrecv, ysem_s, ysem_r, q, j).wait_recv()
        for y in range(nb):
            whole = yrecv[q, y].astype(F32)
            for part in range(2):
                for b in range(bl):
                    v = whole[part * modes:(part + 1) * modes, b * C:(b + 1) * C]
                    head = v[:, :LANES]
                    rest = jnp.concatenate([v[:, LANES:], jnp.zeros((modes, LANES - tail), F32)], axis=1)
                    r1 = ((part * nb + y) * bl + b) * modes
                    r2 = (((1 - part) * nb + y) * bl + b) * modes
                    m1[0, r1:r1 + modes, :] = head
                    m1[1, r1:r1 + modes, :] = rest
                    m2[0, r2:r2 + modes, :] = head if part == 0 else -head
                    m2[1, r2:r2 + modes, :] = rest if part == 0 else -rest
        for copy in weights(q):
            copy.wait()
        s = q % slots

        def one(i, carry):
            at = pl.ds(i, group, stride=modes)
            a1 = jnp.concatenate([m1[0, at, :], m1[1, at, :][:, :tail]], axis=1).astype(BF)
            a2 = jnp.concatenate([m2[0, at, :], m2[1, at, :][:, :tail]], axis=1).astype(BF)
            o = dot(a1, wbuf[s, 0, i]) + dot(a2, wbuf[s, 1, i])
            mo[0, at, :] = o[:, :LANES]
            mo[1, at, :] = jnp.concatenate([o[:, LANES:], jnp.zeros((group, LANES - tail), F32)], axis=1)
            return carry

        lax.fori_loop(0, modes, one, 0, unroll=UNROLL)
        if q + slots < cols:
            for copy in weights(q + slots):
                copy.start()
        for y in range(nb):
            parts = []
            for part in range(2):
                pieces = []
                for b in range(bl):
                    r = ((part * nb + y) * bl + b) * modes
                    pieces += [mo[0, r:r + modes, :], mo[1, r:r + modes, :][:, :tail]]
                parts.append(jnp.concatenate(pieces, axis=1))
            zsend[q, y] = jnp.concatenate(parts, axis=0).astype(BF)
        for j in range(1, nb):
            c = over_ba(zsend, zrecv, zsem_s, zsem_r, q, j)
            c.start()
            sent.append(c)
        zrecv[q, mine] = zsend[q, mine]

    def rows_up(q):
        for j in range(1, nb):
            over_ba(zsend, zrecv, zsem_s, zsem_r, q, j).wait_recv()
        row = dot(up_ref[...], zrecv[q].reshape(nb * 2 * modes, L))
        rsend[q] = row.astype(BF).reshape(n, rows2, L)
        for j in order:
            c = over_ma(rsend, out_ref, rsem_s, rsem_r, q, j)
            c.start()
            sent.append(c)
        out_ref[q, me] = rsend[q, me]

    for t in range(cols + 2):
        if t < cols:
            rows_down(t)
        if 0 <= t - 2 < cols:
            rows_up(t - 2)
        if 0 <= t - 1 < cols:
            mix(t - 1)
    for q in range(cols):
        for j in order:
            over_ma(rsend, out_ref, rsem_s, rsem_r, q, j).wait_recv()
    for c in sent:
        c.wait_send()


UNROLL = 4


def final_kernel(rr_ref, x_ref, last_ref, skip_ref, bias_ref, out_ref, rf):
    bl, step, W, C = x_ref.shape
    cols, n, rows2, L = rr_ref.shape
    rows = rows2 // 2
    K2 = cols * n * 2
    tiles = L // LANES
    g = pl.program_id(0)

    @pl.when(g == 0)
    def _():
        for q in range(cols):
            @pl.loop(0, n)
            def _(d, q=q):
                v = rr_ref[q, d].astype(F32)
                at = pl.ds(pl.multiple_of((q * n + d) * rows2, rows2), rows2)
                for l in range(tiles):
                    rf[l, at, :] = v[:, l * LANES:(l + 1) * LANES]

    for u in range(step):
        h = g * step + u
        r = jnp.concatenate([rf[l, pl.ds(h, K2, stride=rows), :] for l in range(tiles)], axis=1).astype(BF)
        for b in range(bl):
            v = dot(last_ref[...], r[:, b * C:(b + 1) * C]) + dot(x_ref[b, u], skip_ref[...]) + bias_ref[...]
            inner = math.sqrt(2.0 / math.pi) * (v + 0.044715 * (v * v * v))
            out_ref[b, u] = (0.5 * v * (1.0 + jnp.tanh(inner))).astype(BF)


def kernels(n, nb, H, KX, KY, fields, weight_real, weight_imag, skip_weight, out_bias):
    bl, rows, W, C = fields.shape
    modes, cols = weight_real.shape[:2]
    L, K2 = bl * C, 2 * KY
    first, down, up, last = packed_tables(H, W, KX, KY, n, nb)
    vmem = pl.BlockSpec(memory_space=pltpu.VMEM)
    hbm = pl.BlockSpec(memory_space=pl.ANY)
    tiles = L // LANES
    group = 2 * nb * bl
    ma_block = pltpu.VMEM((cols, n, 2 * rows, L), BF)
    ba_block = pltpu.VMEM((cols, nb, 2 * modes, L), BF)
    mix_block = pltpu.VMEM((2, group * modes, LANES), F32)
    dma = pltpu.SemaphoreType.DMA
    rr = pl.pallas_call(
        functools.partial(spectral_kernel, n, nb),
        out_shape=jax.ShapeDtypeStruct((cols, n, 2 * rows, L), BF),
        in_specs=[vmem, hbm, hbm, vmem, vmem, vmem],
        out_specs=vmem,
        scratch_shapes=[
            pltpu.VMEM((tiles, rows * K2, LANES), F32), ma_block, ma_block, ba_block, ba_block,
            mix_block, mix_block, mix_block, ba_block, ba_block, ma_block,
            pltpu.VMEM((min(2, cols), 2, modes, C, C), BF),
            dma((cols, n)), dma((cols, n)), dma((cols, nb)), dma((cols, nb)), dma((cols, nb)),
            dma((cols, nb)), dma((cols, n)), dma((cols, n)), dma((min(2, cols), 2)),
        ],
        compiler_params=pltpu.CompilerParams(
            collective_id=0, has_side_effects=True, vmem_limit_bytes=VMEM_LIMIT
        ),
        name="spectral",
    )(fields, weight_real, weight_imag, first, down, up)
    step = 2 if rows % 2 == 0 else 1
    slab = pl.BlockSpec((bl, step, W, C), lambda g: (0, g, 0, 0))
    return pl.pallas_call(
        final_kernel,
        grid=(rows // step,),
        out_shape=jax.ShapeDtypeStruct(fields.shape, BF),
        in_specs=[vmem, slab, vmem, vmem, vmem],
        out_specs=slab,
        scratch_shapes=[pltpu.VMEM((tiles, K2 * rows, LANES), F32)],
        compiler_params=pltpu.CompilerParams(vmem_limit_bytes=40 * 2**20),
        name="finish",
    )(rr, fields, last, skip_weight, out_bias.reshape(1, C))


def fits(n, nb, fields, weights):
    bl, rows, W, C = fields.shape
    modes, cols = weights.shape[:2]
    whole = 2 * modes * cols * C * 256 * 2
    return (
        rows % 16 == 0 and modes % 8 == 0 and (bl * C) % LANES == 0 and LANES < C < 2 * LANES
        and 2 * nb * bl == 8 and W % LANES == 0 and whole * min(2, cols) // cols < 36 * 2**20
        and cols * n * 2 % LANES == 0
    )


def any_size(n, nb, H, KX, KY, fields, weight_real, weight_imag, skip_weight, out_bias):
    bl, rows, W, C = fields.shape
    modes, cols = weight_real.shape[:2]
    first, down, up, last = packed_tables(H, W, KX, KY, n, nb)
    col = jnp.einsum("qdpw,brwc->dqprbc", first.reshape(cols, n, 2, W), fields, preferred_element_type=F32)
    col = lax.all_to_all(col.astype(BF), "ma", split_axis=0, concat_axis=0, tiled=True)
    spec = jnp.einsum("ypidrh,dqrhbc->ypqbic", down.reshape(nb, 2, modes, n, 2, rows), col, preferred_element_type=F32)
    spec = lax.all_to_all(spec.astype(BF), "ba", split_axis=0, concat_axis=0, tiled=True)
    re, im = spec[:, 0], spec[:, 1]
    mul = functools.partial(jnp.einsum, "yqbic,iqco->yqbio", preferred_element_type=F32)
    mixed = jnp.stack([
        mul(re, weight_real) - mul(im, weight_imag), mul(re, weight_imag) + mul(im, weight_real)
    ], 1)
    mixed = lax.all_to_all(mixed.astype(BF), "ba", split_axis=0, concat_axis=0, tiled=True)
    row = jnp.einsum("drhypi,ypqbic->dqrhbc", up.reshape(n, 2, rows, nb, 2, modes), mixed, preferred_element_type=F32)
    row = lax.all_to_all(row.astype(BF), "ma", split_axis=0, concat_axis=0, tiled=True)
    spectral = jnp.einsum("wqdr,dqrhbc->bhwc", last.reshape(W, cols, n, 2), row, preferred_element_type=F32)
    skip = jnp.dot(fields.reshape(-1, C), skip_weight, preferred_element_type=F32).reshape(spectral.shape)
    return jax.nn.gelu(spectral + skip + out_bias).astype(BF)


def solution(mesh):
    n, nb = mesh.shape["ma"], mesh.shape["ba"]

    def local(fields, weight_real, weight_imag, skip_weight, out_bias):
        sizes = (fields.shape[1] * n, weight_real.shape[0] * nb, weight_real.shape[1] * n)
        run = kernels if fits(n, nb, fields, weight_real) else any_size
        return run(n, nb, *sizes, fields, weight_real, weight_imag, skip_weight, out_bias)

    split = P("ba", "ma", None, None)
    return jax.shard_map(
        local, mesh=mesh, in_specs=(split, split, split, P(), P()), out_specs=split, check_vma=False
    )
```

profile of v0, /device:TPU:0, one launch (start us, length us, event | category | flops | bytes accessed | tf_op | source)
XLA Modules:
  0.0 110.8 jit_solution(13508602644503236108)
XLA Ops:
  0.0 6.0 %copy.10.x_ref = bf16[2,16,256,192]{3,2,1,0:T(8,128)(2,1)} copy(bf16[2,16,256,192]{2,3,1,0:T(8,128)(2,1)} %param.9) | data formatting | bytes 6291456 | tf_op args[0]
  6.0 84.3 %spectral.1.rr_ref = bf16[4,16,32,384]{3,2,1,0:T(8,128)(2,1)} custom-call(bf16[2,16,256,192]{3,2,1,0:T(8,128)(2,1)} %copy.10.x_ref, bf16[56,4,192,192]{3,2,1,0:T(8,128)(2,1)} %wr_ref.1, bf16[56,4,192,192]{3,2,1,0:T(8,128)(2,1)} %wi_ref.1, bf16[128,256]{1,0:T(8,128)(2,1)} %constant.14.first_ref, bf16[224,512]{1,0:T(8,128)(2,1)} %constant.15.down_ref, ...), custom_call_target="tpu_custom_call" | custom-call | tf_op jit(solution)/shard_map/spectral/pallas_call | solution.py:258
  90.3 0.0 copy-start
  90.3 2.2 %copy-done = bf16[2,16,256,192]{3,2,1,0:T(8,128)(2,1)S(1)} copy-done((bf16[2,16,256,192]{3,2,1,0:T(8,128)(2,1)S(1)}, bf16[2,16,256,192]{3,2,1,0:T(8,128)(2,1)}, u32[]{:S(2)}) %copy-start) | copy-done | bytes 3145752
  92.5 0.0 copy-start.2
  92.5 1.4 %copy-done.2 = bf16[4,16,32,384]{3,2,1,0:T(8,128)(2,1)S(1)} copy-done((bf16[4,16,32,384]{3,2,1,0:T(8,128)(2,1)S(1)}, bf16[4,16,32,384]{3,2,1,0:T(8,128)(2,1)}, u32[]{:S(2)}) %copy-start.2) | copy-done | bytes 1572888
  93.9 0.0 copy-start.3
  93.9 0.9 copy-done.3
  94.8 0.0 copy-start.4
  94.8 0.8 copy-done.4
  95.7 0.0 copy-start.5
  95.7 0.7 copy-done.5
  96.3 6.6 %finish.1 = bf16[2,16,256,192]{3,2,1,0:T(8,128)(2,1)S(1)} custom-call(bf16[4,16,32,384]{3,2,1,0:T(8,128)(2,1)S(1)} %copy-done.2, bf16[2,16,256,192]{3,2,1,0:T(8,128)(2,1)S(1)} %copy-done, bf16[256,128]{1,0:T(8,128)(2,1)S(1)} %copy-done.4, bf16[192,192]{1,0:T(8,128)(2,1)S(1)} %copy-done.3, f32[1,192]{1,0:T(1,128)S(1)} %bitcast.1), custom_call_target="tpu_custom_call" | custom-call | tf_op jit(solution)/shard_map/finish/pallas_call | solution.py:277
  102.9 0.0 copy-start.1
  102.9 1.9 %copy-done.1 = bf16[2,16,256,192]{3,2,1,0:T(8,128)(2,1)} copy-done((bf16[2,16,256,192]{3,2,1,0:T(8,128)(2,1)}, bf16[2,16,256,192]{3,2,1,0:T(8,128)(2,1)S(1)}, u32[]{:S(2)}) %copy-start.1) | copy-done | bytes 3145752
  104.8 6.0 %copy.12 = bf16[2,16,256,192]{2,3,1,0:T(8,128)(2,1)} copy(bf16[2,16,256,192]{3,2,1,0:T(8,128)(2,1)} %copy-done.1) | data formatting | bytes 6291456 | tf_op jit(solution)/shard_map/finish/pallas_call | solution.py:277
Async XLA Ops:
  90.3 2.2 %copy-start = (bf16[2,16,256,192]{3,2,1,0:T(8,128)(2,1)S(1)}, bf16[2,16,256,192]{3,2,1,0:T(8,128)(2,1)}, u32[]{:S(2)}) copy-start(bf16[2,16,256,192]{3,2,1,0:T(8,128)(2,1)} %copy.10.x_ref) | copy-start | bytes 9437188
  92.5 1.4 %copy-start.2 = (bf16[4,16,32,384]{3,2,1,0:T(8,128)(2,1)S(1)}, bf16[4,16,32,384]{3,2,1,0:T(8,128)(2,1)}, u32[]{:S(2)}) copy-start(bf16[4,16,32,384]{3,2,1,0:T(8,128)(2,1)} %spectral.1.rr_ref) | copy-start | bytes 4718596
  93.9 0.9 copy-start.3
  94.8 0.8 copy-start.4
  95.7 0.7 copy-start.5
  102.9 1.9 %copy-start.1 = (bf16[2,16,256,192]{3,2,1,0:T(8,128)(2,1)}, bf16[2,16,256,192]{3,2,1,0:T(8,128)(2,1)S(1)}, u32[]{:S(2)}) copy-start(bf16[2,16,256,192]{3,2,1,0:T(8,128)(2,1)S(1)} %finish.1) | copy-start | bytes 9437188
where the time goes:
time: 111 us
  Pallas kernels  90.9 us (82%)
  local copies, waits for them, and re-layouts  19.9 us (18%)
    pallas_call x1, Pallas kernels, kernels(): pl.pallas_call(functools.partial(spectral_kernel, n, nb), out_shape=jax.S...  84.3 us
    unnamed x13, local copies, waits for them, and re-layouts  13.9 us
    pallas_call x1, Pallas kernels, kernels(): pl.pallas_call(final_kernel, grid=(rows // step,), out_shape=jax.ShapeDty...  6.55 us
    pallas_call x1, local copies, waits for them, and re-layouts, kernels(): pl.pallas_call(final_kernel, grid=(rows // step,), out_shape=jax.ShapeDty...  6 us

commit v1 on v0

--- a/solution.py
+++ b/solution.py
@@ -30,7 +30,7 @@
     first = first.reshape(n, cols, 2, W).transpose(1, 0, 2, 3).reshape(2 * KY, W)
     g = np.where(ky == 0, 1.0, 2.0)[:, None] * s
     last = np.stack([cos_w * g, -sin_w * g], 1)
-    last = last.reshape(n, cols, 2, W).transpose(1, 0, 2, 3).reshape(2 * KY, W).T
+    last = last.reshape(n, cols, 2, W).transpose(1, 0, 2, 3).reshape(2 * KY, W)
     i = np.arange(KX)
     kx = np.where(i < KX // 2, i, i + H - KX)
     cos_h, sin_h = angles(kx, np.arange(H), H)
@@ -42,8 +42,8 @@
     return [jnp.asarray(a.astype(np.float32)).astype(BF) for a in (first, down, up, last)]
 
 
-def dot(a, b):
-    return jnp.dot(a, b, preferred_element_type=F32)
+def dot(a, b, over=(1, 0)):
+    return lax.dot_general(a, b, (((over[0],), (over[1],)), ((), ())), preferred_element_type=F32)
 
 
 def spectral_kernel(
@@ -51,7 +51,7 @@
     colf, csend, crecv, ysend, yrecv, m1, m2, mo, zsend, zrecv, rsend, wbuf,
     csem_s, csem_r, ysem_s, ysem_r, zsem_s, zsem_r, rsem_s, rsem_r, wsem,
 ):
-    bl, rows, W, C = x_ref.shape
+    bl, rows, C, W = x_ref.shape
     cols, _, rows2, L = csend.shape
     modes = wbuf.shape[2]
     K2 = first_ref.shape[0]
@@ -101,8 +101,7 @@
 
     @pl.loop(0, rows)
     def _(h):
-        parts = [dot(first_ref[...], x_ref[b, h]) for b in range(bl)]
-        both = jnp.concatenate(parts, axis=1)
+        both = dot(first_ref[...], x_ref[:, h].reshape(L, W), (1, 1))
         for l in range(tiles):
             colf[l, pl.ds(pl.multiple_of(h * K2, K2), K2), :] = both[:, l * LANES:(l + 1) * LANES]
 
@@ -215,8 +214,8 @@
 UNROLL = 4
 
 
-def final_kernel(rr_ref, x_ref, last_ref, skip_ref, bias_ref, out_ref, rf):
-    bl, step, W, C = x_ref.shape
+def final_kernel(rr_ref, x_ref, last_ref, skip_ref, bias_ref, out_ref, rf, turned, biases):
+    bl, step, C, W = x_ref.shape
     cols, n, rows2, L = rr_ref.shape
     rows = rows2 // 2
     K2 = cols * n * 2
@@ -225,6 +224,10 @@
 
     @pl.when(g == 0)
     def _():
+        turned[...] = skip_ref[...].astype(F32).T.astype(BF)
+        wide = jnp.broadcast_to(bias_ref[...], (LANES, C)).T
+        for l in range(W // LANES):
+            biases[:, l * LANES:(l + 1) * LANES] = wide
         for q in range(cols):
             @pl.loop(0, n)
             def _(d, q=q):
@@ -236,8 +239,9 @@
     for u in range(step):
         h = g * step + u
         r = jnp.concatenate([rf[l, pl.ds(h, K2, stride=rows), :] for l in range(tiles)], axis=1).astype(BF)
+        spectral = dot(r, last_ref[...], (0, 0))
         for b in range(bl):
-            v = dot(last_ref[...], r[:, b * C:(b + 1) * C]) + dot(x_ref[b, u], skip_ref[...]) + bias_ref[...]
+            v = spectral[b * C:(b + 1) * C] + dot(turned[...], x_ref[b, u]) + biases[...]
             inner = math.sqrt(2.0 / math.pi) * (v + 0.044715 * (v * v * v))
             out_ref[b, u] = (0.5 * v * (1.0 + jnp.tanh(inner))).astype(BF)
 
@@ -247,6 +251,7 @@
     modes, cols = weight_real.shape[:2]
     L, K2 = bl * C, 2 * KY
     first, down, up, last = packed_tables(H, W, KX, KY, n, nb)
+    fields = fields.transpose(0, 1, 3, 2)
     vmem = pl.BlockSpec(memory_space=pltpu.VMEM)
     hbm = pl.BlockSpec(memory_space=pl.ANY)
     tiles = L // LANES
@@ -273,17 +278,20 @@
         name="spectral",
     )(fields, weight_real, weight_imag, first, down, up)
     step = 2 if rows % 2 == 0 else 1
-    slab = pl.BlockSpec((bl, step, W, C), lambda g: (0, g, 0, 0))
-    return pl.pallas_call(
+    slab = pl.BlockSpec((bl, step, C, W), lambda g: (0, g, 0, 0))
+    out = pl.pallas_call(
         final_kernel,
         grid=(rows // step,),
         out_shape=jax.ShapeDtypeStruct(fields.shape, BF),
         in_specs=[vmem, slab, vmem, vmem, vmem],
         out_specs=slab,
-        scratch_shapes=[pltpu.VMEM((tiles, K2 * rows, LANES), F32)],
-        compiler_params=pltpu.CompilerParams(vmem_limit_bytes=40 * 2**20),
+        scratch_shapes=[
+            pltpu.VMEM((tiles, K2 * rows, LANES), F32), pltpu.VMEM((C, C), BF), pltpu.VMEM((C, W), F32)
+        ],
+        compiler_params=pltpu.CompilerParams(vmem_limit_bytes=VMEM_LIMIT),
         name="finish",
     )(rr, fields, last, skip_weight, out_bias.reshape(1, C))
+    return out.transpose(0, 1, 3, 2)
 
 
 def fits(n, nb, fields, weights):
@@ -313,7 +321,7 @@
     mixed = lax.all_to_all(mixed.astype(BF), "ba", split_axis=0, concat_axis=0, tiled=True)
     row = jnp.einsum("drhypi,ypqbic->dqrhbc", up.reshape(n, 2, rows, nb, 2, modes), mixed, preferred_element_type=F32)
     row = lax.all_to_all(row.astype(BF), "ma", split_axis=0, concat_axis=0, tiled=True)
-    spectral = jnp.einsum("wqdr,dqrhbc->bhwc", last.reshape(W, cols, n, 2), row, preferred_element_type=F32)
+    spectral = jnp.einsum("qdrw,dqrhbc->bhwc", last.reshape(cols, n, 2, W), row, preferred_element_type=F32)
     skip = jnp.dot(fields.reshape(-1, C), skip_weight, preferred_element_type=F32).reshape(spectral.shape)
     return jax.nn.gelu(spectral + skip + out_bias).astype(BF)
 

time: 111 us -> 94.3 us (0.85)
  local copies, waits for them, and re-layouts: 19.9 us -> 0 us
  Pallas kernels: 90.9 us -> 94 us
    unnamed x13 -> x0, local copies, waits for them, and re-layouts: 13.9 us -> none
    pallas_call x1 -> x0, local copies, waits for them, and re-layouts: 6 us -> none  [kernels(): pl.pallas_call(final_kernel, grid=(rows // step,), out_shape=jax.ShapeDty...]
    pallas_call x1, Pallas kernels: 6.55 us -> 9.54 us  [kernels(): pl.pallas_call(final_kernel, grid=(rows // step,), out_shape=jax.ShapeDty...]
where the time goes in v1:
time: 94.3 us; the launch traced here: 94 us
  Pallas kernels  94 us (100%)
    pallas_call x1, Pallas kernels, kernels(): pl.pallas_call(functools.partial(spectral_kernel, n, nb), out_shape=jax.S...  84.5 us
    pallas_call x1, Pallas kernels, kernels(): pl.pallas_call(final_kernel, grid=(rows // step,), out_shape=jax.ShapeDty...  9.54 us

profile of v1, /device:TPU:0, one launch (start us, length us, event | category | flops | bytes accessed | tf_op | source)
XLA Modules:
  0.0 94.0 jit_solution(14715121964950390401)
XLA Ops:
  0.0 84.5 %spectral.1.rr_ref = bf16[4,16,32,384]{3,2,1,0:T(8,128)(2,1)} custom-call(bf16[2,16,192,256]{3,2,1,0:T(8,128)(2,1)} %bitcast.3, bf16[56,4,192,192]{3,2,1,0:T(8,128)(2,1)} %wr_ref.1, bf16[56,4,192,192]{3,2,1,0:T(8,128)(2,1)} %wi_ref.1, bf16[128,256]{1,0:T(8,128)(2,1)} %constant.14.first_ref, bf16[224,512]{1,0:T(8,128)(2,1)} %constant.15.down_ref, ...), custom_call_target="tpu_custom_call" | custom-call | tf_op jit(solution)/shard_map/spectral/pallas_call | solution.py:263
  84.5 9.5 %finish.1 = bf16[2,16,192,256]{3,2,1,0:T(8,128)(2,1)} custom-call(bf16[4,16,32,384]{3,2,1,0:T(8,128)(2,1)} %spectral.1.rr_ref, bf16[2,16,192,256]{3,2,1,0:T(8,128)(2,1)} %bitcast.4, bf16[128,256]{1,0:T(8,128)(2,1)} %constant.17.last_ref, bf16[192,192]{1,0:T(8,128)(2,1)} %skip_ref.1, f32[1,192]{1,0:T(1,128)} %bitcast.5), custom_call_target="tpu_custom_call" | custom-call | tf_op jit(solution)/shard_map/finish/pallas_call | solution.py:282

commit v2 on v1

--- a/solution.py
+++ b/solution.py
@@ -30,7 +30,7 @@
     first = first.reshape(n, cols, 2, W).transpose(1, 0, 2, 3).reshape(2 * KY, W)
     g = np.where(ky == 0, 1.0, 2.0)[:, None] * s
     last = np.stack([cos_w * g, -sin_w * g], 1)
-    last = last.reshape(n, cols, 2, W).transpose(1, 0, 2, 3).reshape(2 * KY, W)
+    last = last.reshape(n, cols, 2, W).transpose(1, 2, 0, 3).reshape(2 * KY, W)
     i = np.arange(KX)
     kx = np.where(i < KX // 2, i, i + H - KX)
     cos_h, sin_h = angles(kx, np.arange(H), H)
@@ -38,7 +38,8 @@
     down = down.reshape(2, nb, modes, 2, n, rows).transpose(1, 0, 2, 4, 3, 5)
     down = down.reshape(2 * KX, 2 * H)
     up = np.stack([np.stack([cos_h, -sin_h], 0), np.stack([sin_h, cos_h], 0)], 0)
-    up = up.reshape(2, 2, nb, modes, n, rows).transpose(4, 0, 5, 2, 1, 3).reshape(2 * H, 2 * KX)
+    up = up.reshape(2, 2, nb, modes, n, 2, rows // 2).transpose(4, 5, 0, 6, 2, 1, 3)
+    up = up.reshape(2 * H, 2 * KX)
     return [jnp.asarray(a.astype(np.float32)).astype(BF) for a in (first, down, up, last)]
 
 
@@ -47,9 +48,10 @@
 
 
 def spectral_kernel(
-    n, nb, x_ref, wr_ref, wi_ref, first_ref, down_ref, up_ref, out_ref,
-    colf, csend, crecv, ysend, yrecv, m1, m2, mo, zsend, zrecv, rsend, wbuf,
-    csem_s, csem_r, ysem_s, ysem_r, zsem_s, zsem_r, rsem_s, rsem_r, wsem,
+    n, nb, x_ref, wr_ref, wi_ref, first_ref, down_ref, up_ref, last_ref, skip_ref, bias_ref, out_ref,
+    colf, csend, crecv, ysend, yrecv, m1, m2, mo, zsend, zrecv, rsend, rrecv, wbuf,
+    xbuf, acc, obuf, rf, turned, biases,
+    csem_s, csem_r, ysem_s, ysem_r, zsem_s, zsem_r, rsem_s, rsem_r, wsem, xsem, osem,
 ):
     bl, rows, C, W = x_ref.shape
     cols, _, rows2, L = csend.shape
@@ -69,9 +71,13 @@
             for p, ref in enumerate((wr_ref, wi_ref))
         ]
 
-    for q in range(min(slots, cols)):
-        for copy in weights(q):
-            copy.start()
+    def loads(g):
+        at = pl.ds(g * PIECE, PIECE)
+        return pltpu.make_async_copy(x_ref.at[:, at], xbuf.at[:, at], xsem.at[g])
+
+    def stores(g):
+        at = pl.ds(g * PIECE, PIECE)
+        return pltpu.make_async_copy(obuf.at[:, at], out_ref.at[:, at], osem.at[g])
 
     barrier = pltpu.get_barrier_semaphore()
     for j in range(1, n):
@@ -97,13 +103,22 @@
             recv_sem=r.at[q, j], device_id={"ba": to}, device_id_type=MESH,
         )
 
+    for g in range(rows // PIECE):
+        loads(g).start()
+    for q in range(min(slots, cols)):
+        for copy in weights(q):
+            copy.start()
+
     order = sorted(range(1, n), key=lambda j: -min(j, n - j))
 
-    @pl.loop(0, rows)
-    def _(h):
-        both = dot(first_ref[...], x_ref[:, h].reshape(L, W), (1, 1))
-        for l in range(tiles):
-            colf[l, pl.ds(pl.multiple_of(h * K2, K2), K2), :] = both[:, l * LANES:(l + 1) * LANES]
+    for g in range(rows // PIECE):
+        loads(g).wait()
+
+        @pl.loop(g * PIECE, (g + 1) * PIECE)
+        def _(h):
+            both = dot(first_ref[...], xbuf[:, h].reshape(L, W), (1, 1))
+            for l in range(tiles):
+                colf[l, pl.ds(pl.multiple_of(h * K2, K2), K2), :] = both[:, l * LANES:(l + 1) * LANES]
 
     sent = []
     for q in range(cols):
@@ -191,59 +206,95 @@
             over_ba(zsend, zrecv, zsem_s, zsem_r, q, j).wait_recv()
         row = dot(up_ref[...], zrecv[q].reshape(nb * 2 * modes, L))
         rsend[q] = row.astype(BF).reshape(n, rows2, L)
-        for j in order:
-            c = over_ma(rsend, out_ref, rsem_s, rsem_r, q, j)
-            c.start()
-            sent.append(c)
-        out_ref[q, me] = rsend[q, me]
-
-    for t in range(cols + 2):
-        if t < cols:
-            rows_down(t)
-        if 0 <= t - 2 < cols:
-            rows_up(t - 2)
-        if 0 <= t - 1 < cols:
-            mix(t - 1)
-    for q in range(cols):
-        for j in order:
-            over_ma(rsend, out_ref, rsem_s, rsem_r, q, j).wait_recv()
-    for c in sent:
-        c.wait_send()
-
-
-UNROLL = 4
-
-
-def final_kernel(rr_ref, x_ref, last_ref, skip_ref, bias_ref, out_ref, rf, turned, biases):
-    bl, step, C, W = x_ref.shape
-    cols, n, rows2, L = rr_ref.shape
-    rows = rows2 // 2
-    K2 = cols * n * 2
-    tiles = L // LANES
-    g = pl.program_id(0)
-
-    @pl.when(g == 0)
-    def _():
+        for half in halves(q):
+            for j in order:
+                c = back(q, j, half)
+                c.start()
+                sent.append(c)
+        rrecv[q, me] = rsend[q, me]
+
+    def halves(q):
+        return (0, 1) if q == cols - 1 else (None,)
+
+    def back(q, j, half):
+        if half is None:
+            return over_ma(rsend, rrecv, rsem_s, rsem_r, q, j)
+        to = lax.rem(me + j, n)
+        at = pl.ds(half * rows, rows)
+        return pltpu.make_async_remote_copy(
+            src_ref=rsend.at[q, to, at], dst_ref=rrecv.at[q, me, at],
+            send_sem=rsem_s.at[q + half, j], recv_sem=rsem_r.at[q + half, j],
+            device_id={"ma": to}, device_id_type=MESH,
+        )
+
+    def pointwise():
         turned[...] = skip_ref[...].astype(F32).T.astype(BF)
         wide = jnp.broadcast_to(bias_ref[...], (LANES, C)).T
         for l in range(W // LANES):
             biases[:, l * LANES:(l + 1) * LANES] = wide
-        for q in range(cols):
+
+        @pl.loop(0, rows)
+        def _(h):
+            for b in range(bl):
+                acc[h, b * C:(b + 1) * C, :] = dot(turned[...], xbuf[b, h]) + biases[...]
+
+    def columns_back(q):
+        final = q == cols - 1
+        for half in halves(q):
+            for j in order:
+                back(q, j, half).wait_recv()
+
             @pl.loop(0, n)
-            def _(d, q=q):
-                v = rr_ref[q, d].astype(F32)
-                at = pl.ds(pl.multiple_of((q * n + d) * rows2, rows2), rows2)
+            def _(d):
+                v = rrecv[q, d].astype(F32) if half is None else rrecv[q, d, half * rows:(half + 1) * rows].astype(F32)
+                size = v.shape[0]
+                at = pl.ds(pl.multiple_of(d * rows2 + (half or 0) * rows, rows), size)
                 for l in range(tiles):
                     rf[l, at, :] = v[:, l * LANES:(l + 1) * LANES]
 
-    for u in range(step):
-        h = g * step + u
-        r = jnp.concatenate([rf[l, pl.ds(h, K2, stride=rows), :] for l in range(tiles)], axis=1).astype(BF)
-        spectral = dot(r, last_ref[...], (0, 0))
-        for b in range(bl):
-            v = spectral[b * C:(b + 1) * C] + dot(turned[...], x_ref[b, u]) + biases[...]
-            inner = math.sqrt(2.0 / math.pi) * (v + 0.044715 * (v * v * v))
-            out_ref[b, u] = (0.5 * v * (1.0 + jnp.tanh(inner))).astype(BF)
+            table = last_ref[q * 2 * n:(q + 1) * 2 * n]
+            for e in (0, 1) if half is None else (half,):
+                for g in range(rows // 2 // PIECE):
+                    @pl.loop(0, PIECE)
+                    def _(i):
+                        low = g * PIECE + i
+                        h = e * (rows // 2) + low
+                        r = jnp.concatenate([
+                            jnp.concatenate([
+                                rf[l, pl.ds(e * rows + part * (rows // 2) + low, n, stride=rows2), :]
+                                for l in range(tiles)
+                            ], axis=1) for part in range(2)
+                        ], axis=0).astype(BF)
+                        spectral = dot(r, table, (0, 0))
+                        for b in range(bl):
+                            v = acc[h, b * C:(b + 1) * C, :] + spectral[b * C:(b + 1) * C]
+                            if not final:
+                                acc[h, b * C:(b + 1) * C, :] = v
+                                continue
+                            inner = math.sqrt(2.0 / math.pi) * (v + 0.044715 * (v * v * v))
+                            obuf[b, h] = (0.5 * v * (1.0 + jnp.tanh(inner))).astype(BF)
+
+                    if final:
+                        stores(e * (rows // 2 // PIECE) + g).start()
+
+    pointwise()
+    for t in range(cols + 1):
+        if t < cols:
+            rows_down(t)
+        if t >= 1:
+            rows_up(t - 1)
+        if t < cols:
+            mix(t)
+    for q in range(cols):
+        columns_back(q)
+    for c in sent:
+        c.wait_send()
+    for g in range(rows // PIECE):
+        stores(g).wait()
+
+
+PIECE = 4
+UNROLL = 4
 
 
 def kernels(n, nb, H, KX, KY, fields, weight_real, weight_imag, skip_weight, out_bias):
@@ -260,37 +311,26 @@
     ba_block = pltpu.VMEM((cols, nb, 2 * modes, L), BF)
     mix_block = pltpu.VMEM((2, group * modes, LANES), F32)
     dma = pltpu.SemaphoreType.DMA
-    rr = pl.pallas_call(
+    out = pl.pallas_call(
         functools.partial(spectral_kernel, n, nb),
-        out_shape=jax.ShapeDtypeStruct((cols, n, 2 * rows, L), BF),
-        in_specs=[vmem, hbm, hbm, vmem, vmem, vmem],
-        out_specs=vmem,
+        out_shape=jax.ShapeDtypeStruct(fields.shape, BF),
+        in_specs=[hbm, hbm, hbm, vmem, vmem, vmem, vmem, vmem, vmem],
+        out_specs=hbm,
         scratch_shapes=[
             pltpu.VMEM((tiles, rows * K2, LANES), F32), ma_block, ma_block, ba_block, ba_block,
-            mix_block, mix_block, mix_block, ba_block, ba_block, ma_block,
+            mix_block, mix_block, mix_block, ba_block, ba_block, ma_block, ma_block,
             pltpu.VMEM((min(2, cols), 2, modes, C, C), BF),
+            pltpu.VMEM((bl, rows, C, W), BF), pltpu.VMEM((rows, L, W), F32), pltpu.VMEM((bl, rows, C, W), BF),
+            pltpu.VMEM((tiles, n * 2 * rows, LANES), F32), pltpu.VMEM((C, C), BF), pltpu.VMEM((C, W), F32),
             dma((cols, n)), dma((cols, n)), dma((cols, nb)), dma((cols, nb)), dma((cols, nb)),
-            dma((cols, nb)), dma((cols, n)), dma((cols, n)), dma((min(2, cols), 2)),
+            dma((cols, nb)), dma((cols + 1, n)), dma((cols + 1, n)), dma((min(2, cols), 2)),
+            dma((rows // PIECE,)), dma((rows // PIECE,)),
         ],
         compiler_params=pltpu.CompilerParams(
             collective_id=0, has_side_effects=True, vmem_limit_bytes=VMEM_LIMIT
         ),
         name="spectral",
-    )(fields, weight_real, weight_imag, first, down, up)
-    step = 2 if rows % 2 == 0 else 1
-    slab = pl.BlockSpec((bl, step, C, W), lambda g: (0, g, 0, 0))
-    out = pl.pallas_call(
-        final_kernel,
-        grid=(rows // step,),
-        out_shape=jax.ShapeDtypeStruct(fields.shape, BF),
-        in_specs=[vmem, slab, vmem, vmem, vmem],
-        out_specs=slab,
-        scratch_shapes=[
-            pltpu.VMEM((tiles, K2 * rows, LANES), F32), pltpu.VMEM((C, C), BF), pltpu.VMEM((C, W), F32)
-        ],
-        compiler_params=pltpu.CompilerParams(vmem_limit_bytes=VMEM_LIMIT),
-        name="finish",
-    )(rr, fields, last, skip_weight, out_bias.reshape(1, C))
+    )(fields, weight_real, weight_imag, first, down, up, last, skip_weight, out_bias.reshape(1, C))
     return out.transpose(0, 1, 3, 2)
 
 
@@ -319,9 +359,10 @@
         mul(re, weight_real) - mul(im, weight_imag), mul(re, weight_imag) + mul(im, weight_real)
     ], 1)
     mixed = lax.all_to_all(mixed.astype(BF), "ba", split_axis=0, concat_axis=0, tiled=True)
-    row = jnp.einsum("drhypi,ypqbic->dqrhbc", up.reshape(n, 2, rows, nb, 2, modes), mixed, preferred_element_type=F32)
+    row = jnp.einsum("derhypi,ypqbic->dqrehbc", up.reshape(n, 2, 2, rows // 2, nb, 2, modes), mixed, preferred_element_type=F32)
     row = lax.all_to_all(row.astype(BF), "ma", split_axis=0, concat_axis=0, tiled=True)
-    spectral = jnp.einsum("qdrw,dqrhbc->bhwc", last.reshape(cols, n, 2, W), row, preferred_element_type=F32)
+    spectral = jnp.einsum("qrdw,dqrehbc->behwc", last.reshape(cols, 2, n, W), row, preferred_element_type=F32)
+    spectral = spectral.reshape(fields.shape)
     skip = jnp.dot(fields.reshape(-1, C), skip_weight, preferred_element_type=F32).reshape(spectral.shape)
     return jax.nn.gelu(spectral + skip + out_bias).astype(BF)
 

time: 94.3 us -> 99.6 us (1.056)
  local copies, waits for them, and re-layouts: 0 us -> 3.88 us
  Pallas kernels: 94 us -> 95.5 us
    pallas_call x1, Pallas kernels: 84.5 us -> 95.5 us  [kernels(): pl.pallas_call(functools.partial(spectral_kernel, n, nb), out_shape=jax.S...]
    pallas_call x1 -> x0, Pallas kernels: 9.54 us -> none  [kernels(): pl.pallas_call(final_kernel, grid=(rows // step,), out_shape=jax.ShapeDty...]
    unnamed x0 -> x1, local copies, waits for them, and re-layouts: none -> 3.88 us
where the time goes in v2:
time: 99.6 us; the launch traced here: 99.4 us
  Pallas kernels  95.5 us (96%)
  local copies, waits for them, and re-layouts  3.88 us (4%)
    pallas_call x1, Pallas kernels, kernels(): pl.pallas_call(functools.partial(spectral_kernel, n, nb), out_shape=jax.S...  95.5 us
    unnamed x1, local copies, waits for them, and re-layouts  3.88 us

profile of v2, /device:TPU:0, one launch (start us, length us, event | category | flops | bytes accessed | tf_op | source)
XLA Modules:
  0.0 99.4 jit_solution(4538069125540271329)
XLA Ops:
  0.0 95.5 %spectral.1 = bf16[2,16,192,256]{3,2,1,0:T(8,128)(2,1)} custom-call(bf16[2,16,192,256]{3,2,1,0:T(8,128)(2,1)} %bitcast.4, bf16[56,4,192,192]{3,2,1,0:T(8,128)(2,1)} %wr_ref.1, bf16[56,4,192,192]{3,2,1,0:T(8,128)(2,1)} %wi_ref.1, bf16[128,256]{1,0:T(8,128)(2,1)} %constant.14.first_ref, bf16[224,512]{1,0:T(8,128)(2,1)} %constant.15.down_ref, ...), custom_call_target="tpu_custom_call" | custom-call | tf_op jit(solution)/shard_map/spectral/pallas_call | solution.py:314
  95.5 3.9 %copy.11 = bf16[2,16,256,192]{2,3,1,0:T(8,128)(2,1)} copy(bf16[2,16,256,192]{2,3,1,0:T(8,128)(2,1)} %bitcast.3) | data formatting | bytes 6291456
